TPU v7x, 256 devices: a whole 4x4x8 slice. The times are simulated.
256 devices in a mesh: row: 32 (over y, z), col: 8 (over x, core).
Axes of the slice: x: 4, y: 4, z: 8, core: 2. Of those that a mesh axis runs over, the one named last changes fastest.
Arguments:
- weights: bfloat16 [2, 8192, 8192], P(None, 'row', 'col'), may hold values from -0.0625 to 0.0625
- preact: float32 [2, 2, 8192], P(None, None, 'row'), may hold values from -2.5 to 2.5
- panel: bfloat16 [2, 64, 8192], P(None, None, 'col'), may hold values from -6 to 6
Outputs:
- basis_out: float32 [2, 64, 8192], P(None, None, 'col')
All inputs are finite; a program needn't handle non-finite values.
Results may differ from a plain program's by a relative error of at most 0.035.
Values may be sent and summed in bfloat16 or wider, within the bound.
No kernel may reach another device: no remote copies, remote signals or barrier semaphores. Data moves between devices by JAX's collectives and lax.ppermute only.
A program may use at most 64 MiB of HBM per device.

v0:
```python
from functools import partial
import jax
import jax.numpy as jnp
from jax import lax
from jax.sharding import PartitionSpec as P

WIDTH = 8192
ITERS = 2


def in_blocks(x, dim, length):
    lengths = x.shape
    tiles = x.reshape(*lengths[:dim], length, lengths[dim] // length, *lengths[dim + 1 :])
    return jnp.moveaxis(tiles, dim, 0)


def sum_at_owner(x, axis, dim):
    tiles = in_blocks(x, dim, lax.axis_size(axis))
    arrived = lax.all_to_all(tiles, axis, split_axis=0, concat_axis=0, tiled=True)
    return arrived.astype(jnp.float32).sum(axis=0)


def from_everyone(x, axis):
    length = lax.axis_size(axis)
    return lax.all_to_all(jnp.broadcast_to(x[None], (length, *x.shape)), axis, 0, 0, tiled=True)


def in_order(tiles, dim):
    tiles = jnp.moveaxis(tiles, 0, dim)
    lengths = tiles.shape
    return tiles.reshape(*lengths[:dim], lengths[dim] * lengths[dim + 1], *lengths[dim + 2 :])


def gathered_copies(x, axis, dim):
    tiles = from_everyone(x, axis)
    return in_order(tiles, dim)


def picked(x, axis, root):
    return lax.dynamic_index_in_dim(lax.all_gather(x, axis), root, 0, keepdims=False)


def over_copies(x, axis):
    everything = from_everyone(x, axis)
    return jnp.sum(everything.astype(jnp.float32), axis=0)


def on_device(weights, preact, panel):
    slopes = 1.0 - jnp.tanh(preact) ** 2
    layers = weights.shape[0]
    span_ratio = lax.axis_size("row") // lax.axis_size("col")
    row_index = lax.axis_index("row")
    current = panel
    basis_out = panel.astype(jnp.float32)
    for iteration in range(ITERS):
        cotangent = None
        for layer_at in range(layers):
            partial_out = jnp.einsum(
                "bki,oi->bko", current, weights[layer_at], preferred_element_type=jnp.float32
            )
            summed = sum_at_owner(partial_out.astype(jnp.bfloat16), "col", 1)
            scaled = (slopes[:, layer_at, None, :] * summed).astype(jnp.bfloat16)
            if layer_at + 1 < layers:
                spread = gathered_copies(scaled, "row", 2)
                current = lax.all_to_all(spread, "col", split_axis=2, concat_axis=1, tiled=True)
            else:
                cotangent = gathered_copies(scaled, "col", 1)
        image_panel = None
        for layer_at in reversed(range(layers)):
            weighted = (slopes[:, layer_at, None, :] * cotangent).astype(jnp.bfloat16)
            partial_in = jnp.einsum(
                "bko,oi->bki", weighted, weights[layer_at], preferred_element_type=jnp.float32
            )
            if layer_at == 0:
                pieces = sum_at_owner(partial_in.astype(jnp.bfloat16), "row", 2).astype(
                    jnp.bfloat16
                )
                image_panel = gathered_copies(pieces, "row", 2)
            else:
                pieces = sum_at_owner(partial_in.astype(jnp.bfloat16), "row", 2).astype(
                    jnp.bfloat16
                )
                gathered = gathered_copies(pieces, "row", 2)
                chosen = picked(gathered, "col", row_index // span_ratio)
                width_row = cotangent.shape[2]
                cotangent = lax.dynamic_slice_in_dim(
                    chosen, row_index % span_ratio * width_row, width_row, 2
                )
        local_gram = jnp.einsum(
            "bkw,bjw->bkj", image_panel, image_panel, preferred_element_type=jnp.float32
        )
        gram_sum = over_copies(local_gram.astype(jnp.bfloat16), "col").astype(jnp.float32)
        factor = jnp.linalg.cholesky(gram_sum / WIDTH)
        basis_out = jax.vmap(partial(jax.scipy.linalg.solve_triangular, lower=True))(
            factor, image_panel.astype(jnp.float32)
        )
        current = basis_out.astype(jnp.bfloat16)
    return basis_out


def solution(mesh):
    return jax.shard_map(
        on_device,
        mesh=mesh,
        in_specs=(P(None, "row", "col"), P(None, None, "row"), P(None, None, "col")),
        out_specs=P(None, None, "col"),
        check_vma=False,
    )
```

profile of v0, /device:TPU:1, one launch (start us, length us, event | category | flops | bytes accessed | tf_op | source)
XLA Modules:
  0.0 452.3 jit_solution(6569241820050055485)
XLA Ops:
  6.5 0.9 copy-done
  7.5 1.3 fusion
  9.5 6.5 %all-to-all-start = ((bf16[8,2,8,256]{3,2,1,0:T(8,128)(2,1)}), bf16[8,2,8,256]{3,2,1,0:T(8,128)(2,1)S(1)}, u32[]{:S(2)}, u32[]{:S(2)}) async-start(bf16[8,2,8,256]{3,2,1,0:T(8,128)(2,1)} %bitcast.159), calls=%async_computation | async-start | bytes 131072 | tf_op jit(solution)/shard_map/all_to_all | solution.py:19
  15.9 0.7 multiply_subtract_fusion
  16.6 4.2 all-to-all-done
  20.9 20.0 %all_to_all.126 = bf16[32,2,8,256]{3,2,1,0:T(8,128)(2,1)S(1)} all-to-all(bf16[32,2,8,256]{3,2,1,0:T(8,128)(2,1)S(1)} %broadcast_in_dim.24), channel_id=1, replica_groups=mesh['row'=32,'col'=8] {'row'}, dimensions={0} | all-to-all | bytes 524288 | tf_op jit(solution)/shard_map/all_to_all | solution.py:25
  40.8 6.8 %copy.135 = bf16[2,8,32,256]{1,0,3,2:T(2,128)(2,1)} copy(bf16[2,8,32,256]{3,1,0,2:T(8,128)(2,1)S(1)} %bitcast.184) | data formatting | bytes 524288 | tf_op jit(solution)/shard_map/reshape | solution.py:31
  47.7 5.8 %reshape.89 = bf16[8,2,8192]{2,1,0:T(2,128)(2,1)S(1)} reshape(bf16[8192,2,8]{2,1,0:T(2,128)(2,1)} %bitcast.166) | data formatting | bytes 524288
  53.4 12.6 %all_to_all.127 = bf16[8,2,8192]{2,1,0:T(2,128)(2,1)S(1)} all-to-all(bf16[8,2,8192]{2,1,0:T(2,128)(2,1)S(1)} %reshape.89), channel_id=1, replica_groups=mesh['row'=32,'col'=8] {'col'}, dimensions={0} | all-to-all | bytes 524288 | tf_op jit(solution)/shard_map/all_to_all | solution.py:65
  66.1 5.9 %reshape.90 = bf16[8192,2,8]{2,1,0:T(2,128)(2,1)} reshape(bf16[8,2,8192]{2,1,0:T(2,128)(2,1)S(1)} %all_to_all.127) | data formatting | bytes 524288
  72.0 9.0 %copy.94 = bf16[2,8,8,1024]{3,1,2,0:T(8,128)(2,1)S(1)} copy(bf16[2,8,8,1024]{1,0,3,2:T(2,128)(2,1)} %bitcast.167) | data formatting | bytes 524288 | tf_op jit(solution)/shard_map/all_to_all | solution.py:65
  81.9 4.3 all-to-all-start.3
  86.2 4.9 %all-to-all-done.3 = bf16[8,2,8,256]{3,2,1,0:T(8,128)(2,1)S(1)} async-done(((bf16[8,2,8,256]{3,2,1,0:T(8,128)(2,1)}), bf16[8,2,8,256]{3,2,1,0:T(8,128)(2,1)S(1)}, u32[]{:S(2)}, u32[]{:S(2)}) %all-to-all-start.3) | async-done | bytes 65568 | tf_op jit(solution)/shard_map/all_to_all | solution.py:19
  91.1 8.0 %all_to_all.128 = bf16[8,2,8,256]{3,2,1,0:T(8,128)(2,1)S(1)} all-to-all(bf16[8,2,8,256]{3,2,1,0:T(8,128)(2,1)S(1)} %broadcast_in_dim.25), channel_id=1, replica_groups=mesh['row'=32,'col'=8] {'col'}, dimensions={0} | all-to-all | bytes 131072 | tf_op jit(solution)/shard_map/all_to_all | solution.py:25
  100.1 13.6 %all_to_all.129 = bf16[32,2,2048]{2,1,0:T(2,128)(2,1)S(1)} all-to-all(bf16[32,2,2048]{2,1,0:T(2,128)(2,1)S(1)} %reshape.91), channel_id=1, replica_groups=mesh['row'=32,'col'=8] {'row'}, dimensions={0} | all-to-all | bytes 524288 | tf_op jit(solution)/shard_map/all_to_all | solution.py:19
  114.7 15.7 %all_to_all.130 = bf16[32,2,2048]{2,1,0:T(2,128)(2,1)S(1)} all-to-all(bf16[32,2,2048]{2,1,0:T(2,128)(2,1)S(1)} %reshape.93), channel_id=1, replica_groups=mesh['row'=32,'col'=8] {'row'}, dimensions={0} | all-to-all | bytes 524288 | tf_op jit(solution)/shard_map/all_to_all | solution.py:25
  130.8 0.9 copy.100
  131.8 25.4 %all-gather.3.cloned.1.call-done = bf16[8,2,64,1024]{3,2,1,0:T(8,128)(2,1)} async-done(((bf16[1,2,64,1024]{3,2,1,0:T(8,128)(2,1)}), bf16[8,2,64,1024]{3,2,1,0:T(8,128)(2,1)}) %all-gather.3.cloned.1.call-update) | async-done | bytes 2097168 | tf_op jit(solution)/shard_map/all_gather | solution.py:40
  157.2 1.2 convolution_convert_fusion.3
  159.1 19.3 %all_to_all.131 = bf16[32,2,2048]{2,1,0:T(2,128)(2,1)S(1)} all-to-all(bf16[32,2,2048]{2,1,0:T(2,128)(2,1)S(1)} %reshape.95), channel_id=1, replica_groups=mesh['row'=32,'col'=8] {'row'}, dimensions={0} | all-to-all | bytes 524288 | tf_op jit(solution)/shard_map/all_to_all | solution.py:19
  179.5 16.1 %all_to_all.132 = bf16[32,2,2048]{2,1,0:T(2,128)(2,1)S(1)} all-to-all(bf16[32,2,2048]{2,1,0:T(2,128)(2,1)S(1)} %reshape.97), channel_id=1, replica_groups=mesh['row'=32,'col'=8] {'row'}, dimensions={0} | all-to-all | bytes 524288 | tf_op jit(solution)/shard_map/all_to_all | solution.py:25
  196.4 0.9 reshape.99
  197.3 7.1 %all-to-all-start.9 = ((bf16[8,2,4096]{2,1,0:T(2,128)(2,1)}), bf16[8,2,4096]{2,1,0:T(2,128)(2,1)S(1)}, u32[]{:S(2)}, u32[]{:S(2)}) async-start(bf16[8,2,4096]{2,1,0:T(2,128)(2,1)} %reshape.99), calls=%async_computation.9 | async-start | bytes 262144 | tf_op jit(solution)/shard_map/all_to_all | solution.py:25
  204.5 5.0 %all-to-all-done.9 = bf16[8,2,4096]{2,1,0:T(2,128)(2,1)S(1)} async-done(((bf16[8,2,4096]{2,1,0:T(2,128)(2,1)}), bf16[8,2,4096]{2,1,0:T(2,128)(2,1)S(1)}, u32[]{:S(2)}, u32[]{:S(2)}) %all-to-all-start.9) | async-done | bytes 131104 | tf_op jit(solution)/shard_map/all_to_all | solution.py:25
  210.0 11.7 %custom-call.8 = f32[2,64,64]{2,1,0:T(8,128)S(1)} custom-call(f32[2,64,64]{2,1,0:T(8,128)S(1)} %fusion.36), custom_call_target="Cholesky" | custom-call | tf_op jit(solution)/shard_map/jit(cholesky)/cholesky | solution.py:93
  222.0 9.8 %custom-call.9 = f32[2,1,64,64]{2,3,1,0:T(8,128)S(1)} custom-call(f32[2,1,64,64]{3,2,1,0:T(8,128)S(1)} %select_bitcast_fusion.1), custom_call_target="InvertDiagBlocksLowerTriangular" | custom-call | tf_op jit(solution)/shard_map/vmap(jit(_solve_triangular))/triangular_solve | solution.py:94
  232.8 8.1 %all_to_all.133 = bf16[8,2,8,256]{3,2,1,0:T(8,128)(2,1)S(1)} all-to-all(bf16[8,2,8,256]{3,2,1,0:T(8,128)(2,1)S(1)} %bitcast.186), channel_id=1, replica_groups=mesh['row'=32,'col'=8] {'col'}, dimensions={0} | all-to-all | bytes 131072 | tf_op jit(solution)/shard_map/all_to_all | solution.py:19
  241.0 13.7 %all_to_all.134 = bf16[32,2,8,256]{3,2,1,0:T(8,128)(2,1)S(1)} all-to-all(bf16[32,2,8,256]{3,2,1,0:T(8,128)(2,1)S(1)} %broadcast_in_dim.29), channel_id=1, replica_groups=mesh['row'=32,'col'=8] {'row'}, dimensions={0} | all-to-all | bytes 524288 | tf_op jit(solution)/shard_map/all_to_all | solution.py:25
  254.6 6.8 %copy.136 = bf16[2,8,32,256]{1,0,3,2:T(2,128)(2,1)} copy(bf16[2,8,32,256]{3,1,0,2:T(8,128)(2,1)S(1)} %bitcast.185) | data formatting | bytes 524288 | tf_op jit(solution)/shard_map/reshape | solution.py:31
  261.4 5.8 %reshape.101 = bf16[8,2,8192]{2,1,0:T(2,128)(2,1)S(1)} reshape(bf16[8192,2,8]{2,1,0:T(2,128)(2,1)} %bitcast.168) | data formatting | bytes 524288
  267.2 12.6 %all_to_all.135 = bf16[8,2,8192]{2,1,0:T(2,128)(2,1)S(1)} all-to-all(bf16[8,2,8192]{2,1,0:T(2,128)(2,1)S(1)} %reshape.101), channel_id=1, replica_groups=mesh['row'=32,'col'=8] {'col'}, dimensions={0} | all-to-all | bytes 524288 | tf_op jit(solution)/shard_map/all_to_all | solution.py:65
  279.8 5.9 %reshape.102 = bf16[8192,2,8]{2,1,0:T(2,128)(2,1)} reshape(bf16[8,2,8192]{2,1,0:T(2,128)(2,1)S(1)} %all_to_all.135) | data formatting | bytes 524288
  285.8 8.9 %copy.113 = bf16[2,8,8,1024]{3,1,2,0:T(8,128)(2,1)S(1)} copy(bf16[2,8,8,1024]{1,0,3,2:T(2,128)(2,1)} %bitcast.169) | data formatting | bytes 524288 | tf_op jit(solution)/shard_map/all_to_all | solution.py:65
  295.0 8.3 %all_to_all.136 = bf16[8,2,8,256]{3,2,1,0:T(8,128)(2,1)S(1)} all-to-all(bf16[8,2,8,256]{3,2,1,0:T(8,128)(2,1)S(1)} %bitcast.187), channel_id=1, replica_groups=mesh['row'=32,'col'=8] {'col'}, dimensions={0} | all-to-all | bytes 131072 | tf_op jit(solution)/shard_map/all_to_all | solution.py:19
  303.3 8.0 %all_to_all.137 = bf16[8,2,8,256]{3,2,1,0:T(8,128)(2,1)S(1)} all-to-all(bf16[8,2,8,256]{3,2,1,0:T(8,128)(2,1)S(1)} %broadcast_in_dim.30), channel_id=1, replica_groups=mesh['row'=32,'col'=8] {'col'}, dimensions={0} | all-to-all | bytes 131072 | tf_op jit(solution)/shard_map/all_to_all | solution.py:25
  312.3 13.6 %all_to_all.138 = bf16[32,2,2048]{2,1,0:T(2,128)(2,1)S(1)} all-to-all(bf16[32,2,2048]{2,1,0:T(2,128)(2,1)S(1)} %reshape.103), channel_id=1, replica_groups=mesh['row'=32,'col'=8] {'row'}, dimensions={0} | all-to-all | bytes 524288 | tf_op jit(solution)/shard_map/all_to_all | solution.py:19
  326.9 15.7 %all_to_all.139 = bf16[32,2,2048]{2,1,0:T(2,128)(2,1)S(1)} all-to-all(bf16[32,2,2048]{2,1,0:T(2,128)(2,1)S(1)} %reshape.105), channel_id=1, replica_groups=mesh['row'=32,'col'=8] {'row'}, dimensions={0} | all-to-all | bytes 524288 | tf_op jit(solution)/shard_map/all_to_all | solution.py:25
  343.0 0.9 copy.119
  343.9 25.5 %all-gather.5.cloned.1.call-done = bf16[8,2,64,1024]{3,2,1,0:T(8,128)(2,1)} async-done(((bf16[1,2,64,1024]{3,2,1,0:T(8,128)(2,1)}), bf16[8,2,64,1024]{3,2,1,0:T(8,128)(2,1)}) %all-gather.5.cloned.1.call-update) | async-done | bytes 2097168 | tf_op jit(solution)/shard_map/all_gather | solution.py:40
  369.4 1.2 convolution_convert_fusion
  371.3 19.3 %all_to_all.140 = bf16[32,2,2048]{2,1,0:T(2,128)(2,1)S(1)} all-to-all(bf16[32,2,2048]{2,1,0:T(2,128)(2,1)S(1)} %reshape.107), channel_id=1, replica_groups=mesh['row'=32,'col'=8] {'row'}, dimensions={0} | all-to-all | bytes 524288 | tf_op jit(solution)/shard_map/all_to_all | solution.py:19
  391.6 16.1 %all_to_all.141 = bf16[32,2,2048]{2,1,0:T(2,128)(2,1)S(1)} all-to-all(bf16[32,2,2048]{2,1,0:T(2,128)(2,1)S(1)} %reshape.109), channel_id=1, replica_groups=mesh['row'=32,'col'=8] {'row'}, dimensions={0} | all-to-all | bytes 524288 | tf_op jit(solution)/shard_map/all_to_all | solution.py:25
  408.5 0.9 reshape.111
  409.4 7.0 %all-to-all-start.19 = ((bf16[8,2,4096]{2,1,0:T(2,128)(2,1)}), bf16[8,2,4096]{2,1,0:T(2,128)(2,1)S(1)}, u32[]{:S(2)}, u32[]{:S(2)}) async-start(bf16[8,2,4096]{2,1,0:T(2,128)(2,1)} %reshape.111), calls=%async_computation.19 | async-start | bytes 262144 | tf_op jit(solution)/shard_map/all_to_all | solution.py:25
  416.7 5.0 %all-to-all-done.19 = bf16[8,2,4096]{2,1,0:T(2,128)(2,1)S(1)} async-done(((bf16[8,2,4096]{2,1,0:T(2,128)(2,1)}), bf16[8,2,4096]{2,1,0:T(2,128)(2,1)S(1)}, u32[]{:S(2)}, u32[]{:S(2)}) %all-to-all-start.19) | async-done | bytes 131104 | tf_op jit(solution)/shard_map/all_to_all | solution.py:25
  422.2 11.7 %custom-call.10 = f32[2,64,64]{2,1,0:T(8,128)S(1)} custom-call(f32[2,64,64]{2,1,0:T(8,128)S(1)} %fusion.34), custom_call_target="Cholesky" | custom-call | tf_op jit(solution)/shard_map/jit(cholesky)/cholesky | solution.py:93
  434.2 9.8 %custom-call.11 = f32[2,1,64,64]{2,3,1,0:T(8,128)S(1)} custom-call(f32[2,1,64,64]{3,2,1,0:T(8,128)S(1)} %select_bitcast_fusion), custom_call_target="InvertDiagBlocksLowerTriangular" | custom-call | tf_op jit(solution)/shard_map/vmap(jit(_solve_triangular))/triangular_solve | solution.py:94
  444.0 1.4 fusion.12
  (98 shorter events, 14.5 us)
Async XLA Ops:
  6.5 1.0 copy-start
  9.5 11.3 %all-to-all-start = ((bf16[8,2,8,256]{3,2,1,0:T(8,128)(2,1)}), bf16[8,2,8,256]{3,2,1,0:T(8,128)(2,1)S(1)}, u32[]{:S(2)}, u32[]{:S(2)}) async-start(bf16[8,2,8,256]{3,2,1,0:T(8,128)(2,1)} %bitcast.159), calls=%async_computation | async-start | bytes 131072 | tf_op jit(solution)/shard_map/all_to_all | solution.py:19
  72.0 9.0 %copy-start.1 = (bf16[2,256,1024]{2,1,0:T(8,128)(2,1)S(1)}, bf16[2,256,1024]{2,1,0:T(8,128)(2,1)}, u32[]{:S(2)}) copy-start(bf16[2,256,1024]{2,1,0:T(8,128)(2,1)} %param.6) | copy-start | bytes 3145732
  81.9 9.2 %all-to-all-start.3 = ((bf16[8,2,8,256]{3,2,1,0:T(8,128)(2,1)}), bf16[8,2,8,256]{3,2,1,0:T(8,128)(2,1)S(1)}, u32[]{:S(2)}, u32[]{:S(2)}) async-start(bf16[8,2,8,256]{3,2,1,0:T(8,128)(2,1)} %bitcast.158), calls=%async_computation.3 | async-start | bytes 131072 | tf_op jit(solution)/shard_map/all_to_all | solution.py:19
  86.2 71.0 %all-gather.3.cloned.1.call-start = ((), (), s32[]{:S(2)}) async-start(), calls=%async_computation.20 | async-start | bytes 2359296 | tf_op jit(solution)/shard_map/all_gather | solution.py:40
  197.3 12.3 %all-to-all-start.9 = ((bf16[8,2,4096]{2,1,0:T(2,128)(2,1)}), bf16[8,2,4096]{2,1,0:T(2,128)(2,1)S(1)}, u32[]{:S(2)}, u32[]{:S(2)}) async-start(bf16[8,2,4096]{2,1,0:T(2,128)(2,1)} %reshape.99), calls=%async_computation.9 | async-start | bytes 262144 | tf_op jit(solution)/shard_map/all_to_all | solution.py:25
  204.3 165.1 %all-gather.5.cloned.1.call-start = ((), (), s32[]{:S(2)}) async-start(), calls=%async_computation.21 | async-start | bytes 2359296 | tf_op jit(solution)/shard_map/all_gather | solution.py:40
  409.4 12.3 %all-to-all-start.19 = ((bf16[8,2,4096]{2,1,0:T(2,128)(2,1)}), bf16[8,2,4096]{2,1,0:T(2,128)(2,1)S(1)}, u32[]{:S(2)}, u32[]{:S(2)}) async-start(bf16[8,2,4096]{2,1,0:T(2,128)(2,1)} %reshape.111), calls=%async_computation.19 | async-start | bytes 262144 | tf_op jit(solution)/shard_map/all_to_all | solution.py:25
Sparse Core Ops, SparseCore 0:
  131.9 25.3 all-gather.2
  344.0 25.3 all-gather.4
where the time goes:
time: 454 us; the launch traced here: 452 us
  blocking collectives  221 us (49%)
  local copies, waits for them, and re-layouts  70 us (15%)
  waiting for transfers between devices  70 us (15%)
  other arithmetic  45 us (10%)
  starting transfers between devices  24.9 us (5%)
  between operations  14.1 us (3%)
  matrix products  7.79 us (2%)
    all_to_all x8, blocking collectives, from_everyone(): lax.all_to_all(jnp.broadcast_to(x[None], (length, *x.shape)), axis, 0, 0,...  113 us
    all_to_all x6, blocking collectives, sum_at_owner(): lax.all_to_all(tiles, axis, split_axis=0, concat_axis=0, tiled=True)  82.2 us
    all_gather x2, waiting for transfers between devices, picked(): lax.all_gather(x, axis)  50.9 us
    unnamed x34, local copies, waits for them, and re-layouts  32.9 us
    all_to_all x2, blocking collectives, on_device(): lax.all_to_all(spread, 'col', split_axis=2, concat_axis=1, tiled=True)  25.2 us
    another operation x7, other arithmetic, on_device(): factor = jnp.linalg.cholesky(gram_sum / WIDTH)  23.8 us
    another operation x5, other arithmetic, on_device(): jax.vmap(partial(jax.scipy.linalg.solve_triangular, lower=True))  19.8 us
    all_to_all x2, local copies, waits for them, and re-layouts, on_device(): lax.all_to_all(spread, 'col', split_axis=2, concat_axis=1, tiled=True)  17.9 us
  transfers between devices with their start and end apart: 6, of which 6 were waited for; matrix products, arithmetic and copies ran while one was open for 0% of the time, Pallas kernels for 0%

commit v1 on v0

--- a/solution.py
+++ b/solution.py
@@ -62,7 +62,12 @@
             scaled = (slopes[:, layer_at, None, :] * summed).astype(jnp.bfloat16)
             if layer_at + 1 < layers:
                 spread = gathered_copies(scaled, "row", 2)
-                current = lax.all_to_all(spread, "col", split_axis=2, concat_axis=1, tiled=True)
+                current = jnp.concatenate(
+                    lax.all_to_all(
+                        jnp.stack(jnp.split(spread, lax.axis_size("col"), axis=2)), "col", 0, 0
+                    ),
+                    axis=1,
+                )
             else:
                 cotangent = gathered_copies(scaled, "col", 1)
         image_panel = None

time: 454 us -> 399 us (0.88)
  local copies, waits for them, and re-layouts: 70 us -> 15.3 us
    unnamed x34 -> x44, local copies, waits for them, and re-layouts: 32.9 us -> 9.64 us
    all_to_all x2 -> x0, local copies, waits for them, and re-layouts: 17.9 us -> none  [on_device(): lax.all_to_all(spread, 'col', split_axis=2, concat_axis=1, tiled=True)]
    reshape x4, local copies, waits for them, and re-layouts: 14.1 us -> 0.44 us  [in_order(): tiles.reshape(*lengths[:dim], lengths[dim] * lengths[dim + 1], *lengths[d...]
where the time goes in v1:
time: 399 us; the launch traced here: 398 us
  blocking collectives  221 us (55%)
  waiting for transfers between devices  70 us (18%)
  other arithmetic  45 us (11%)
  starting transfers between devices  24.9 us (6%)
  local copies, waits for them, and re-layouts  15.3 us (4%)
  between operations  14.2 us (4%)
  matrix products  7.77 us (2%)
    all_to_all x8, blocking collectives, from_everyone(): lax.all_to_all(jnp.broadcast_to(x[None], (length, *x.shape)), axis, 0, 0,...  113 us
    all_to_all x6, blocking collectives, sum_at_owner(): lax.all_to_all(tiles, axis, split_axis=0, concat_axis=0, tiled=True)  82.2 us
    all_gather x2, waiting for transfers between devices, picked(): lax.all_gather(x, axis)  50.9 us
    all_to_all x2, blocking collectives, on_device(): lax.all_to_all(jnp.stack(jnp.split(spread, lax.axis_size('col'), axis=2))...  25.2 us
    another operation x7, other arithmetic, on_device(): factor = jnp.linalg.cholesky(gram_sum / WIDTH)  23.8 us
    another operation x5, other arithmetic, on_device(): jax.vmap(partial(jax.scipy.linalg.solve_triangular, lower=True))  19.8 us
    all_to_all x2, starting transfers between devices, from_everyone(): lax.all_to_all(jnp.broadcast_to(x[None], (length, *x.shape)), axis, 0, 0,...  14.1 us
    all_to_all x2, starting transfers between devices, sum_at_owner(): lax.all_to_all(tiles, axis, split_axis=0, concat_axis=0, tiled=True)  10.7 us
  transfers between devices with their start and end apart: 6, of which 6 were waited for; matrix products, arithmetic and copies ran while one was open for 0% of the time, Pallas kernels for 0%

profile of v1, /device:TPU:1, one launch (start us, length us, event | category | flops | bytes accessed | tf_op | source)
XLA Modules:
  0.0 397.8 jit_solution(15190778601595388620)
XLA Ops:
  6.5 0.9 copy-done
  7.5 1.3 fusion
  8.8 0.6 copy.188
  9.5 6.5 %all-to-all-start = ((bf16[8,2,8,256]{3,2,1,0:T(8,128)(2,1)}), bf16[8,2,8,256]{3,2,1,0:T(8,128)(2,1)S(1)}, u32[]{:S(2)}, u32[]{:S(2)}) async-start(bf16[8,2,8,256]{3,2,1,0:T(8,128)(2,1)} %bitcast.223), calls=%async_computation | async-start | bytes 131072 | tf_op jit(solution)/shard_map/all_to_all | solution.py:19
  15.9 0.7 multiply_subtract_fusion
  16.6 4.2 %all-to-all-done = bf16[8,2,8,256]{3,2,1,0:T(8,128)(2,1)S(1)} async-done(((bf16[8,2,8,256]{3,2,1,0:T(8,128)(2,1)}), bf16[8,2,8,256]{3,2,1,0:T(8,128)(2,1)S(1)}, u32[]{:S(2)}, u32[]{:S(2)}) %all-to-all-start) | async-done | bytes 65568 | tf_op jit(solution)/shard_map/all_to_all | solution.py:19
  20.9 20.0 %all_to_all.100 = bf16[32,2,8,256]{3,2,1,0:T(8,128)(2,1)S(1)} all-to-all(bf16[32,2,8,256]{3,2,1,0:T(8,128)(2,1)S(1)} %broadcast_in_dim.24), channel_id=1, replica_groups=mesh['row'=32,'col'=8] {'row'}, dimensions={0} | all-to-all | bytes 524288 | tf_op jit(solution)/shard_map/all_to_all | solution.py:25
  41.0 12.6 %all_to_all.101 = bf16[8,2,8,1024]{3,2,1,0:T(8,128)(2,1)S(1)} all-to-all(bf16[8,2,8,1024]{3,2,1,0:T(8,128)(2,1)S(1)} %constant_dynamic-update-slice_fusion), channel_id=1, replica_groups=mesh['row'=32,'col'=8] {'col'}, dimensions={0} | all-to-all | bytes 524288 | tf_op jit(solution)/shard_map/all_to_all | solution.py:66
  53.9 0.6 copy.187
  54.5 4.3 %all-to-all-start.3 = ((bf16[8,2,8,256]{3,2,1,0:T(8,128)(2,1)}), bf16[8,2,8,256]{3,2,1,0:T(8,128)(2,1)S(1)}, u32[]{:S(2)}, u32[]{:S(2)}) async-start(bf16[8,2,8,256]{3,2,1,0:T(8,128)(2,1)} %bitcast.222), calls=%async_computation.3 | async-start | bytes 131072 | tf_op jit(solution)/shard_map/all_to_all | solution.py:19
  58.8 4.9 %all-to-all-done.3 = bf16[8,2,8,256]{3,2,1,0:T(8,128)(2,1)S(1)} async-done(((bf16[8,2,8,256]{3,2,1,0:T(8,128)(2,1)}), bf16[8,2,8,256]{3,2,1,0:T(8,128)(2,1)S(1)}, u32[]{:S(2)}, u32[]{:S(2)}) %all-to-all-start.3) | async-done | bytes 65568 | tf_op jit(solution)/shard_map/all_to_all | solution.py:19
  63.7 8.0 %all_to_all.102 = bf16[8,2,8,256]{3,2,1,0:T(8,128)(2,1)S(1)} all-to-all(bf16[8,2,8,256]{3,2,1,0:T(8,128)(2,1)S(1)} %broadcast_in_dim.25), channel_id=1, replica_groups=mesh['row'=32,'col'=8] {'col'}, dimensions={0} | all-to-all | bytes 131072 | tf_op jit(solution)/shard_map/all_to_all | solution.py:25
  72.3 0.4 reshape.105
  72.7 13.6 %all_to_all.103 = bf16[32,2,2048]{2,1,0:T(2,128)(2,1)S(1)} all-to-all(bf16[32,2,2048]{2,1,0:T(2,128)(2,1)S(1)} %reshape.105), channel_id=1, replica_groups=mesh['row'=32,'col'=8] {'row'}, dimensions={0} | all-to-all | bytes 524288 | tf_op jit(solution)/shard_map/all_to_all | solution.py:19
  86.9 0.4 reshape.107
  87.3 15.7 %all_to_all.104 = bf16[32,2,2048]{2,1,0:T(2,128)(2,1)S(1)} all-to-all(bf16[32,2,2048]{2,1,0:T(2,128)(2,1)S(1)} %reshape.107), channel_id=1, replica_groups=mesh['row'=32,'col'=8] {'row'}, dimensions={0} | all-to-all | bytes 524288 | tf_op jit(solution)/shard_map/all_to_all | solution.py:25
  103.4 0.9 copy.121
  104.4 25.4 %all-gather.3.cloned.1.call-done = bf16[8,2,64,1024]{3,2,1,0:T(8,128)(2,1)} async-done(((bf16[1,2,64,1024]{3,2,1,0:T(8,128)(2,1)}), bf16[8,2,64,1024]{3,2,1,0:T(8,128)(2,1)}) %all-gather.3.cloned.1.call-update) | async-done | bytes 2097168 | tf_op jit(solution)/shard_map/all_gather | solution.py:40
  129.8 1.2 convolution_convert_fusion.3
  131.4 0.4 reshape.109
  131.8 19.3 %all_to_all.105 = bf16[32,2,2048]{2,1,0:T(2,128)(2,1)S(1)} all-to-all(bf16[32,2,2048]{2,1,0:T(2,128)(2,1)S(1)} %reshape.109), channel_id=1, replica_groups=mesh['row'=32,'col'=8] {'row'}, dimensions={0} | all-to-all | bytes 524288 | tf_op jit(solution)/shard_map/all_to_all | solution.py:19
  152.1 16.1 %all_to_all.106 = bf16[32,2,2048]{2,1,0:T(2,128)(2,1)S(1)} all-to-all(bf16[32,2,2048]{2,1,0:T(2,128)(2,1)S(1)} %reshape.111), channel_id=1, replica_groups=mesh['row'=32,'col'=8] {'row'}, dimensions={0} | all-to-all | bytes 524288 | tf_op jit(solution)/shard_map/all_to_all | solution.py:25
  169.0 0.9 reshape.113
  169.9 7.0 %all-to-all-start.9 = ((bf16[8,2,4096]{2,1,0:T(2,128)(2,1)}), bf16[8,2,4096]{2,1,0:T(2,128)(2,1)S(1)}, u32[]{:S(2)}, u32[]{:S(2)}) async-start(bf16[8,2,4096]{2,1,0:T(2,128)(2,1)} %reshape.113), calls=%async_computation.9 | async-start | bytes 262144 | tf_op jit(solution)/shard_map/all_to_all | solution.py:25
  177.2 5.0 %all-to-all-done.9 = bf16[8,2,4096]{2,1,0:T(2,128)(2,1)S(1)} async-done(((bf16[8,2,4096]{2,1,0:T(2,128)(2,1)}), bf16[8,2,4096]{2,1,0:T(2,128)(2,1)S(1)}, u32[]{:S(2)}, u32[]{:S(2)}) %all-to-all-start.9) | async-done | bytes 131104 | tf_op jit(solution)/shard_map/all_to_all | solution.py:25
  182.7 11.7 %custom-call.8 = f32[2,64,64]{2,1,0:T(8,128)S(1)} custom-call(f32[2,64,64]{2,1,0:T(8,128)S(1)} %fusion.38), custom_call_target="Cholesky" | custom-call | tf_op jit(solution)/shard_map/jit(cholesky)/cholesky | solution.py:98
  194.7 9.8 %custom-call.9 = f32[2,1,64,64]{2,3,1,0:T(8,128)S(1)} custom-call(f32[2,1,64,64]{3,2,1,0:T(8,128)S(1)} %select_bitcast_fusion.1), custom_call_target="InvertDiagBlocksLowerTriangular" | custom-call | tf_op jit(solution)/shard_map/vmap(jit(_solve_triangular))/triangular_solve | solution.py:99
  204.5 0.6 convolution_convert_fusion.2
  205.5 8.1 %all_to_all.107 = bf16[8,2,8,256]{3,2,1,0:T(8,128)(2,1)S(1)} all-to-all(bf16[8,2,8,256]{3,2,1,0:T(8,128)(2,1)S(1)} %bitcast.262), channel_id=1, replica_groups=mesh['row'=32,'col'=8] {'col'}, dimensions={0} | all-to-all | bytes 131072 | tf_op jit(solution)/shard_map/all_to_all | solution.py:19
  213.6 13.8 %all_to_all.108 = bf16[32,2,8,256]{3,2,1,0:T(8,128)(2,1)S(1)} all-to-all(bf16[32,2,8,256]{3,2,1,0:T(8,128)(2,1)S(1)} %broadcast_in_dim.29), channel_id=1, replica_groups=mesh['row'=32,'col'=8] {'row'}, dimensions={0} | all-to-all | bytes 524288 | tf_op jit(solution)/shard_map/all_to_all | solution.py:25
  227.6 12.6 %all_to_all.109 = bf16[8,2,8,1024]{3,2,1,0:T(8,128)(2,1)S(1)} all-to-all(bf16[8,2,8,1024]{3,2,1,0:T(8,128)(2,1)S(1)} %constant_dynamic-update-slice_fusion.8), channel_id=1, replica_groups=mesh['row'=32,'col'=8] {'col'}, dimensions={0} | all-to-all | bytes 524288 | tf_op jit(solution)/shard_map/all_to_all | solution.py:66
  240.5 8.3 %all_to_all.110 = bf16[8,2,8,256]{3,2,1,0:T(8,128)(2,1)S(1)} all-to-all(bf16[8,2,8,256]{3,2,1,0:T(8,128)(2,1)S(1)} %bitcast.263), channel_id=1, replica_groups=mesh['row'=32,'col'=8] {'col'}, dimensions={0} | all-to-all | bytes 131072 | tf_op jit(solution)/shard_map/all_to_all | solution.py:19
  248.8 8.0 %all_to_all.111 = bf16[8,2,8,256]{3,2,1,0:T(8,128)(2,1)S(1)} all-to-all(bf16[8,2,8,256]{3,2,1,0:T(8,128)(2,1)S(1)} %broadcast_in_dim.30), channel_id=1, replica_groups=mesh['row'=32,'col'=8] {'col'}, dimensions={0} | all-to-all | bytes 131072 | tf_op jit(solution)/shard_map/all_to_all | solution.py:25
  257.4 0.4 reshape.115
  257.8 13.6 %all_to_all.112 = bf16[32,2,2048]{2,1,0:T(2,128)(2,1)S(1)} all-to-all(bf16[32,2,2048]{2,1,0:T(2,128)(2,1)S(1)} %reshape.115), channel_id=1, replica_groups=mesh['row'=32,'col'=8] {'row'}, dimensions={0} | all-to-all | bytes 524288 | tf_op jit(solution)/shard_map/all_to_all | solution.py:19
  272.0 0.4 reshape.117
  272.4 15.7 %all_to_all.113 = bf16[32,2,2048]{2,1,0:T(2,128)(2,1)S(1)} all-to-all(bf16[32,2,2048]{2,1,0:T(2,128)(2,1)S(1)} %reshape.117), channel_id=1, replica_groups=mesh['row'=32,'col'=8] {'row'}, dimensions={0} | all-to-all | bytes 524288 | tf_op jit(solution)/shard_map/all_to_all | solution.py:25
  288.5 0.9 copy.139
  289.4 25.5 %all-gather.5.cloned.1.call-done = bf16[8,2,64,1024]{3,2,1,0:T(8,128)(2,1)} async-done(((bf16[1,2,64,1024]{3,2,1,0:T(8,128)(2,1)}), bf16[8,2,64,1024]{3,2,1,0:T(8,128)(2,1)}) %all-gather.5.cloned.1.call-update) | async-done | bytes 2097168 | tf_op jit(solution)/shard_map/all_gather | solution.py:40
  314.9 1.2 convolution_convert_fusion
  316.8 19.3 %all_to_all.114 = bf16[32,2,2048]{2,1,0:T(2,128)(2,1)S(1)} all-to-all(bf16[32,2,2048]{2,1,0:T(2,128)(2,1)S(1)} %reshape.119), channel_id=1, replica_groups=mesh['row'=32,'col'=8] {'row'}, dimensions={0} | all-to-all | bytes 524288 | tf_op jit(solution)/shard_map/all_to_all | solution.py:19
  337.1 16.1 %all_to_all.115 = bf16[32,2,2048]{2,1,0:T(2,128)(2,1)S(1)} all-to-all(bf16[32,2,2048]{2,1,0:T(2,128)(2,1)S(1)} %reshape.121), channel_id=1, replica_groups=mesh['row'=32,'col'=8] {'row'}, dimensions={0} | all-to-all | bytes 524288 | tf_op jit(solution)/shard_map/all_to_all | solution.py:25
  354.1 0.9 reshape.123
  355.0 7.1 %all-to-all-start.19 = ((bf16[8,2,4096]{2,1,0:T(2,128)(2,1)}), bf16[8,2,4096]{2,1,0:T(2,128)(2,1)S(1)}, u32[]{:S(2)}, u32[]{:S(2)}) async-start(bf16[8,2,4096]{2,1,0:T(2,128)(2,1)} %reshape.123), calls=%async_computation.19 | async-start | bytes 262144 | tf_op jit(solution)/shard_map/all_to_all | solution.py:25
  362.2 5.0 %all-to-all-done.19 = bf16[8,2,4096]{2,1,0:T(2,128)(2,1)S(1)} async-done(((bf16[8,2,4096]{2,1,0:T(2,128)(2,1)}), bf16[8,2,4096]{2,1,0:T(2,128)(2,1)S(1)}, u32[]{:S(2)}, u32[]{:S(2)}) %all-to-all-start.19) | async-done | bytes 131104 | tf_op jit(solution)/shard_map/all_to_all | solution.py:25
  367.7 11.7 %custom-call.10 = f32[2,64,64]{2,1,0:T(8,128)S(1)} custom-call(f32[2,64,64]{2,1,0:T(8,128)S(1)} %fusion.36), custom_call_target="Cholesky" | custom-call | tf_op jit(solution)/shard_map/jit(cholesky)/cholesky | solution.py:98
  379.7 9.8 %custom-call.11 = f32[2,1,64,64]{2,3,1,0:T(8,128)S(1)} custom-call(f32[2,1,64,64]{3,2,1,0:T(8,128)S(1)} %select_bitcast_fusion), custom_call_target="InvertDiagBlocksLowerTriangular" | custom-call | tf_op jit(solution)/shard_map/vmap(jit(_solve_triangular))/triangular_solve | solution.py:99
  389.5 1.4 fusion.12
  (108 shorter events, 10.7 us)
Async XLA Ops:
  6.5 1.0 copy-start
  6.5 47.0 %copy-start.1 = (bf16[2,256,1024]{2,1,0:T(8,128)(2,1)S(1)}, bf16[2,256,1024]{2,1,0:T(8,128)(2,1)}, u32[]{:S(2)}) copy-start(bf16[2,256,1024]{2,1,0:T(8,128)(2,1)} %param.6) | copy-start | bytes 3145732
  9.5 11.3 %all-to-all-start = ((bf16[8,2,8,256]{3,2,1,0:T(8,128)(2,1)}), bf16[8,2,8,256]{3,2,1,0:T(8,128)(2,1)S(1)}, u32[]{:S(2)}, u32[]{:S(2)}) async-start(bf16[8,2,8,256]{3,2,1,0:T(8,128)(2,1)} %bitcast.223), calls=%async_computation | async-start | bytes 131072 | tf_op jit(solution)/shard_map/all_to_all | solution.py:19
  54.5 9.2 %all-to-all-start.3 = ((bf16[8,2,8,256]{3,2,1,0:T(8,128)(2,1)}), bf16[8,2,8,256]{3,2,1,0:T(8,128)(2,1)S(1)}, u32[]{:S(2)}, u32[]{:S(2)}) async-start(bf16[8,2,8,256]{3,2,1,0:T(8,128)(2,1)} %bitcast.222), calls=%async_computation.3 | async-start | bytes 131072 | tf_op jit(solution)/shard_map/all_to_all | solution.py:19
  58.8 71.0 %all-gather.3.cloned.1.call-start = ((), (), s32[]{:S(2)}) async-start(), calls=%async_computation.20 | async-start | bytes 2359296 | tf_op jit(solution)/shard_map/all_gather | solution.py:40
  169.9 12.3 %all-to-all-start.9 = ((bf16[8,2,4096]{2,1,0:T(2,128)(2,1)}), bf16[8,2,4096]{2,1,0:T(2,128)(2,1)S(1)}, u32[]{:S(2)}, u32[]{:S(2)}) async-start(bf16[8,2,4096]{2,1,0:T(2,128)(2,1)} %reshape.113), calls=%async_computation.9 | async-start | bytes 262144 | tf_op jit(solution)/shard_map/all_to_all | solution.py:25
  177.0 138.0 %all-gather.5.cloned.1.call-start = ((), (), s32[]{:S(2)}) async-start(), calls=%async_computation.21 | async-start | bytes 2359296 | tf_op jit(solution)/shard_map/all_gather | solution.py:40
  355.0 12.3 %all-to-all-start.19 = ((bf16[8,2,4096]{2,1,0:T(2,128)(2,1)}), bf16[8,2,4096]{2,1,0:T(2,128)(2,1)S(1)}, u32[]{:S(2)}, u32[]{:S(2)}) async-start(bf16[8,2,4096]{2,1,0:T(2,128)(2,1)} %reshape.123), calls=%async_computation.19 | async-start | bytes 262144 | tf_op jit(solution)/shard_map/all_to_all | solution.py:25
Sparse Core Ops, SparseCore 0:
  104.5 25.3 all-gather.2
  289.6 25.3 all-gather.4
